TPU v7x, 32 devices: a whole 2x2x4 slice. The times are simulated.
32 devices in a mesh: replica: 2 (over core), model: 4 (over y, x), copy: 4 (over z).
Axes of the slice: x: 2, y: 2, z: 4, core: 2. Of those that a mesh axis runs over, the one named last changes fastest.
Arguments:
- slope_up: bfloat16 [8, 1280, 5120], P(('copy', 'replica'), None, 'model'), parts along dimension 0, may hold values from -0.875 to 0.875
- slope_down: bfloat16 [8, 5120, 1280], P(('copy', 'replica'), 'model'), parts along dimension 0, may hold values from -0.875 to 0.875
- slope_norm: bfloat16 [8, 1280], P(('copy', 'replica')), parts along dimension 0, may hold values from -8 to 8
- param_up: float32 [5120, 5120], P(('copy', 'replica'), 'model'), parts along dimension 0, may hold values from -0.25 to 0.25
- param_down: float32 [20480, 1280], P(('copy', 'model'), 'replica'), parts along dimension 0, may hold values from -0.125 to 0.125
- param_norm: float32 [5120], P(('copy', 'replica')), parts along dimension 0, may hold values from 0.25 to 1.75
Outputs:
- half_up: bfloat16 [5120, 5120], P('copy', 'model'), parts along dimension 0
- half_down: bfloat16 [20480, 1280], P(('copy', 'model')), parts along dimension 0
- half_norm: bfloat16 [5120], P('copy'), parts along dimension 0
- next_up: float32 [5120, 5120], P(('copy', 'replica'), 'model'), parts along dimension 0
- next_down: float32 [20480, 1280], P(('copy', 'model'), 'replica'), parts along dimension 0
- next_norm: float32 [5120], P(('copy', 'replica')), parts along dimension 0
There are 4 independent parts, one for each index of `copy`. A program takes and returns all parts, laid end to end along the dimension named above; each array names one. Nothing has to cross between parts.
All inputs are finite; a program needn't handle non-finite values.
Results may differ from a plain program's by a relative error of at most 0.011.
Values may be sent and summed in bfloat16 or wider, within the bound.
A program may use at most 128 MiB of HBM per device.

v0:
```python
import jax
import jax.numpy as jnp
from jax import lax
from jax.sharding import PartitionSpec as P

learn_rate = 0.5


def shards(slope_up, slope_down, slope_norm, param_up, param_down, param_norm):
    mean_up, mean_down = (
        lax.psum_scatter(
            slope_up[0].astype(jnp.float32).astype(jnp.bfloat16),
            "replica",
            scatter_dimension=0,
            tiled=True,
        ).astype(jnp.float32),
        lax.psum_scatter(
            slope_down[0].astype(jnp.float32).astype(jnp.bfloat16),
            "replica",
            scatter_dimension=1,
            tiled=True,
        ).astype(jnp.float32),
    )
    whole_norm = lax.psum(slope_norm[0].astype(jnp.float32), "replica")
    place = lax.axis_index("replica")
    mean_norm = lax.dynamic_slice_in_dim(
        whole_norm, place * param_norm.shape[0], param_norm.shape[0]
    )
    mean_rate = lax.axis_size("replica") ** (-0.5)
    mean_up = mean_up * mean_rate
    mean_down = mean_down * mean_rate
    mean_norm = mean_norm * mean_rate
    own_up, own_down, slope_up_norm, slope_down_norm = lax.psum(
        (
            jnp.sum(param_up * param_up, axis=1, keepdims=True),
            jnp.sum(param_down * param_down, axis=0, keepdims=True),
            jnp.sum(mean_up * mean_up, axis=1, keepdims=True),
            jnp.sum(mean_down * mean_down, axis=0, keepdims=True),
        ),
        "model",
    )
    mean_up = mean_up * (jnp.sqrt(own_up) * lax.rsqrt(slope_up_norm + 1e-06))
    mean_down = mean_down * (jnp.sqrt(own_down) * lax.rsqrt(slope_down_norm + 1e-06))
    next_up = param_up - learn_rate * mean_up
    next_down = param_down - learn_rate * mean_down
    next_norm = param_norm - learn_rate * mean_norm
    half_up, half_down, half_norm = (
        lax.all_gather(next_up.astype(jnp.bfloat16), "replica", axis=0, tiled=True),
        lax.all_gather(next_down.astype(jnp.bfloat16), "replica", axis=1, tiled=True),
        lax.all_gather(next_norm.astype(jnp.bfloat16), "replica", axis=0, tiled=True),
    )
    return (half_up, half_down, half_norm, next_up, next_down, next_norm)


def solution(mesh):
    return jax.shard_map(
        shards,
        mesh=mesh,
        in_specs=(
            P(("copy", "replica"), None, "model"),
            P(("copy", "replica"), "model", None),
            P(("copy", "replica"), None),
            P(("copy", "replica"), "model"),
            P(("copy", "model"), "replica"),
            P(("copy", "replica")),
        ),
        out_specs=(
            P("copy", "model"),
            P(("copy", "model"), None),
            P("copy"),
            P(("copy", "replica"), "model"),
            P(("copy", "model"), "replica"),
            P(("copy", "replica")),
        ),
        check_vma=False,
    )
```

profile of v0, /device:TPU:0, one launch (start us, length us, event | category | flops | bytes accessed | tf_op | source)
XLA Modules:
  0.0 104.4 jit_solution(8484387778861719061)
XLA Ops:
  7.2 0.0 reduce-scatter.7.cloned.1.call-start
  7.2 5.7 %copy.12 = bf16[1280,1280]{0,1:T(8,128)(2,1)} copy(bf16[1280,1280]{1,0:T(8,128)(2,1)} %bitcast.5) | data formatting | bytes 6553600
  12.9 0.0 reduce-scatter.7.cloned.1.call-update
  12.9 0.0 reduce-scatter.5.cloned.1.call-start
  12.9 0.0 copy-start
  13.0 0.7 reduce-scatter.5.cloned.1.call-update
  13.6 0.0 all-gather.6.cloned.1.call-start
  13.7 2.4 %multiply_reduce_fusion.1 = f32[640]{0:T(1024)S(1)} fusion(f32[640,1280]{1,0:T(8,128)} %param.9), kind=kLoop, calls=%fused_computation.13 | loop fusion | flops 1637760 | bytes 3279360 | tf_op jit(solution)/shard_map/reduce_sum | solution.py:35
  16.1 0.0 copy-done
  16.2 0.3 multiply_reduce_fusion
  16.5 10.6 %reduce-scatter.7.cloned.1.call-done = bf16[640,1280]{1,0:T(8,128)(2,1)} async-done(((bf16[1280,1280]{1,0:T(8,128)(2,1)}), bf16[640,1280]{1,0:T(8,128)(2,1)}) %reduce-scatter.7.cloned.1.call-update) | async-done | bytes 1638416
  27.1 2.8 %copy.13 = bf16[1280,640]{1,0:T(8,128)(2,1)S(1)} copy(bf16[1280,640]{0,1:T(8,128)(2,1)} %bitcast.7) | data formatting | bytes 3276800
  30.0 0.5 fusion.5
  30.5 11.6 %reduce-scatter.5.cloned.1.call-done = bf16[640,1280]{1,0:T(8,128)(2,1)} async-done(((bf16[1280,1280]{1,0:T(8,128)(2,1)}), bf16[640,1280]{1,0:T(8,128)(2,1)}) %reduce-scatter.5.cloned.1.call-update) | async-done | bytes 1638416 | tf_op jit(solution)/shard_map/reduce_scatter | solution.py:11
  42.0 1.9 %fusion.1 = f32[640]{0:T(1024)S(1)} fusion(bf16[640,1280]{1,0:T(8,128)(2,1)} %reduce-scatter.5.cloned.1.call-done), kind=kLoop, calls=%fused_computation.5 | loop fusion | flops 3276160 | bytes 1640960 | tf_op jit(solution)/shard_map/reduce_sum | solution.py:37
  44.0 16.3 %all-reduce = (f32[640,1]{0,1:T(1,128)S(1)}, f32[640,1]{0,1:T(1,128)S(1)}, f32[1,640]{1,0:T(1,128)S(1)}, f32[1,640]{1,0:T(1,128)S(1)}) all-reduce(f32[640,1]{0,1:T(1,128)S(1)} %broadcast_in_dim.13, f32[640,1]{0,1:T(1,128)S(1)} %broadcast_in_dim.12, ...), channel_id=1, replica_groups=mesh['replica'=2,'model'=4,'copy'=4] {'model'}, use_global_device_ids=true, to_apply=%region_4.0 | all-reduce | flops 2560 | bytes 20480 | tf_op jit(solution)/shard_map/psum | solution.py:33
  60.3 0.0 copy-start.1
  60.3 4.8 %fusion.9 = (bf16[1280,640]{1,0:T(8,128)(2,1)}, f32[1280,640]{1,0:T(8,128)}) fusion(f32[1280,640]{1,0:T(8,128)} %param.10, f32[640]{0:T(1024)S(1)} %multiply_reduce_fusion.2, bf16[1280,640]{1,0:T(8,128)(2,1)S(1)} %copy.13), kind=kLoop, calls=%fused_computation.19 | loop fusion | flops 4096000 | bytes 9832960 | tf_op jit(solution)/shard_map/convert_element_type | solution.py:49
  65.1 0.0 all-gather.6.cloned.1.call-update
  65.1 0.0 all-gather.4.cloned.1.call-start
  65.2 0.0 copy-done.1
  65.2 0.0 copy-start.3
  65.2 0.0 copy-start.4
  65.2 4.7 %fusion.11 = (bf16[640,1280]{1,0:T(8,128)(2,1)}, f32[640,1280]{1,0:T(8,128)}) fusion(f32[640,1280]{1,0:T(8,128)} %param.9, f32[640]{0:T(1024)S(1)} %multiply_reduce_fusion.3, bf16[640,1280]{1,0:T(8,128)(2,1)S(1)} %copy-done.1), kind=kLoop, calls=%fused_computation.20 | loop fusion | flops 4096000 | bytes 9832960 | tf_op jit(solution)/shard_map/convert_element_type | solution.py:48
  69.9 0.0 all-gather.4.cloned.1.call-update
  70.0 0.0 copy-done.3
  70.0 2.5 %psum.39 = f32[1280]{0:T(1024)S(1)} all-reduce(f32[1280]{0:T(1024)S(1)} %convert_reduce_fusion), channel_id=1, replica_groups=mesh['replica'=2,'model'=4,'copy'=4] {'replica'}, use_global_device_ids=true, to_apply=%region_10.0 | all-reduce | flops 1280 | bytes 10240 | tf_op jit(solution)/shard_map/psum | solution.py:24
  72.5 0.0 copy-done.4
  72.5 0.7 fusion.8
  73.2 1.8 %all-gather = bf16[2,1,640]{2,1,0:T(2,128)(2,1)S(1)} all-gather(bf16[1,1,640]{2,1,0:T(2,128)(2,1)S(1)} %reshape.19), channel_id=1, replica_groups=mesh['replica'=2,'model'=4,'copy'=4] {'replica'}, dimensions={0}, use_global_device_ids=true | all-gather | bytes 3840 | tf_op jit(solution)/shard_map/all_gather | solution.py:50
  75.1 0.6 reshape.20
  75.7 1.0 all-gather.6.cloned.1.call-done
  76.6 15.5 %all-gather.4.cloned.1.call-done = bf16[1280,1280]{1,0:T(8,128)(2,1)} async-done(((bf16[640,1280]{1,0:T(8,128)(2,1)}), bf16[1280,1280]{1,0:T(8,128)(2,1)}) %all-gather.4.cloned.1.call-update) | async-done | bytes 3276816 | tf_op jit(solution)/shard_map/all_gather | solution.py:48
  92.1 0.0 copy-start.2
  92.1 4.0 %copy.16 = bf16[1280,1280]{1,0:T(8,128)(2,1)} copy(bf16[1280,1280]{1,0:T(8,128)(2,1)} %all-gather.4.cloned.1.call-done) | data formatting | bytes 6553600
  96.1 0.0 copy-done.2
  96.1 1.7 %copy.17 = bf16[1280,1280]{1,0:T(8,128)(2,1)} copy(bf16[1280,1280]{1,0:T(8,128)(2,1)S(1)} %copy-done.2) | data formatting | bytes 6553600
  (9 shorter events, 0.1 us)
Async XLA Ops:
  7.2 20.0 %reduce-scatter.7.cloned.1.call-start = ((), (), s32[]{:S(2)}) async-start(), calls=%async_computation.5 | async-start | bytes 4915200
  12.9 29.1 %reduce-scatter.5.cloned.1.call-start = ((), (), s32[]{:S(2)}) async-start(), calls=%async_computation.2 | async-start | bytes 4915200 | tf_op jit(solution)/shard_map/reduce_scatter | solution.py:11
  12.9 3.2 %copy-start = (f32[1280,640]{1,0:T(8,128)S(1)}, f32[1280,640]{1,0:T(8,128)}, u32[]{:S(2)}) copy-start(f32[1280,640]{1,0:T(8,128)} %param.10) | copy-start | bytes 9830404
  13.6 63.0 %all-gather.6.cloned.1.call-start = ((), (), s32[]{:S(2)}) async-start(), calls=%async_computation.4 | async-start | bytes 4915200 | tf_op jit(solution)/shard_map/all_gather | solution.py:49
  60.3 4.9 %copy-start.1 = (bf16[640,1280]{1,0:T(8,128)(2,1)S(1)}, bf16[640,1280]{1,0:T(8,128)(2,1)}, u32[]{:S(2)}) copy-start(bf16[640,1280]{1,0:T(8,128)(2,1)} %reduce-scatter.5.cloned.1.call-done) | copy-start | bytes 4915204
  65.1 27.0 %all-gather.4.cloned.1.call-start = ((), (), s32[]{:S(2)}) async-start(), calls=%async_computation.3 | async-start | bytes 4915200 | tf_op jit(solution)/shard_map/all_gather | solution.py:48
  65.2 4.8 %copy-start.3 = (bf16[1,1280]{1,0:T(2,128)(2,1)S(1)}, bf16[1,1280]{1,0:T(2,128)(2,1)}, u32[]{:S(2)}) copy-start(bf16[1,1280]{1,0:T(2,128)(2,1)} %param.8) | copy-start | bytes 7684
  65.2 7.3 %copy-start.4 = (f32[640]{0:T(1024)S(1)}, f32[640]{0:T(1024)}, u32[]{:S(2)}) copy-start(f32[640]{0:T(1024)} %param.11) | copy-start | bytes 7684
  92.1 4.0 %copy-start.2 = (bf16[1280,1280]{1,0:T(8,128)(2,1)S(1)}, bf16[1280,1280]{1,0:T(8,128)(2,1)}, u32[]{:S(2)}) copy-start(bf16[1280,1280]{1,0:T(8,128)(2,1)} %all-gather.6.cloned.1.call-done) | copy-start | bytes 9830404
Sparse Core Ops, SparseCore 0:
  13.0 14.0 reduce-scatter.6
  29.4 12.6 reduce-scatter.4
  65.2 11.3 all-gather.5
  78.6 13.4 all-gather.3
where the time goes:
time: 105 us; the launch traced here: 104 us
  waiting for transfers between devices  39.4 us (38%)
  blocking collectives  20.6 us (20%)
  other arithmetic  15.5 us (15%)
  local copies, waits for them, and re-layouts  14.9 us (14%)
  between operations  13.9 us (13%)
    psum x1, blocking collectives, shards(): lax.psum((jnp.sum(param_up * param_up, axis=1, keepdims=True), jnp.sum(pa...  16.3 us
    all_gather x1, waiting for transfers between devices, shards(): lax.all_gather(next_up.astype(jnp.bfloat16), 'replica', axis=0, tiled=True)  15.5 us
    unnamed x16, local copies, waits for them, and re-layouts  14.8 us
    reduce_scatter x1, waiting for transfers between devices, shards(): lax.psum_scatter(slope_up[0].astype(jnp.float32).astype(jnp.bfloat16), 'r...  11.6 us
    unnamed x5, waiting for transfers between devices  11.4 us
    convert_element_type x1, other arithmetic, shards(): next_down.astype(jnp.bfloat16)  4.78 us
    convert_element_type x1, other arithmetic, shards(): next_up.astype(jnp.bfloat16)  4.72 us
    psum x1, blocking collectives, shards(): whole_norm = lax.psum(slope_norm[0].astype(jnp.float32), 'replica')  2.5 us
  transfers between devices with their start and end apart: 4, of which 4 were waited for; matrix products, arithmetic and copies ran while one was open for 12% of the time, Pallas kernels for 0%

commit v1 on v0

--- a/solution.py
+++ b/solution.py
@@ -1,6 +1,10 @@
+import functools
+
 import jax
 import jax.numpy as jnp
 from jax import lax
+from jax.experimental import pallas as pl
+from jax.experimental.pallas import tpu as pltpu
 from jax.sharding import PartitionSpec as P
 
 learn_rate = 0.5
@@ -52,9 +56,369 @@
     return (half_up, half_down, half_norm, next_up, next_down, next_norm)
 
 
+MESH = pl.DeviceIdType.MESH
+LANES = 128
+ROWS = 32
+
+
+def update_kernel(
+    replicas,
+    models,
+    slope_up,
+    slope_down,
+    slope_norm,
+    param_up,
+    param_down,
+    param_norm,
+    half_up,
+    half_down,
+    half_norm,
+    next_up,
+    next_down,
+    next_norm,
+    own_up,
+    peer_up,
+    own_down,
+    peer_down,
+    own_vec,
+    peer_vec,
+    peer_gain,
+    sum_vec,
+    whole_vec,
+    part,
+    got,
+    square,
+    spread,
+    load_sem,
+    pair_send,
+    pair_recv,
+    norm_send,
+    norm_recv,
+):
+    me = lax.axis_index("replica")
+    other = 1 - me
+    spot = lax.axis_index("model")
+    share, inner = param_up.shape
+    depth = param_down.shape[0]
+    up_chunks = share // LANES
+    down_rows = 256 if depth % 256 == 0 else LANES
+    down_chunks = depth // down_rows
+    mine = pl.multiple_of(me * share, LANES)
+    theirs = pl.multiple_of(other * share, LANES)
+    rate = replicas ** (-0.5)
+    f32 = jnp.float32
+
+    loads = {}
+
+    def load(name, source, target):
+        copy = pltpu.make_async_copy(source, target, load_sem.at[len(loads)])
+        copy.start()
+        loads[name] = copy
+
+    pairs = {}
+
+    def push(name, source, target):
+        copy = pltpu.make_async_remote_copy(
+            source,
+            target,
+            pair_send.at[len(pairs)],
+            pair_recv.at[len(pairs)],
+            device_id={"replica": other},
+            device_id_type=MESH,
+        )
+        copy.start()
+        pairs[name] = copy
+
+    def up_rows(c):
+        return pl.ds(c * LANES, LANES)
+
+    def down_part(c):
+        return pl.ds(c * down_rows, down_rows)
+
+    load("pu", param_up, next_up)
+    load("pd", param_down, next_down)
+    for c in range(up_chunks):
+        load(
+            ("up", c),
+            slope_up.at[0, pl.ds(mine + c * LANES, LANES), :],
+            own_up.at[up_rows(c), :],
+        )
+    for c in range(down_chunks):
+        load(
+            ("down", c),
+            slope_down.at[0, down_part(c), pl.ds(mine, share)],
+            own_down.at[down_part(c), :],
+        )
+    load("sn", slope_norm, own_vec)
+
+    barrier = pltpu.get_barrier_semaphore()
+    pl.semaphore_signal(
+        barrier, inc=1, device_id={"replica": other}, device_id_type=MESH
+    )
+    for k in range(1, models):
+        pl.semaphore_signal(
+            barrier,
+            inc=1,
+            device_id={"model": lax.rem(spot + k, models)},
+            device_id_type=MESH,
+        )
+    pl.semaphore_wait(barrier, models)
+
+    for c in range(up_chunks):
+        push(
+            ("up", c),
+            slope_up.at[0, pl.ds(theirs + c * LANES, LANES), :],
+            peer_up.at[up_rows(c), :],
+        )
+    for c in range(down_chunks):
+        push(
+            ("down", c),
+            slope_down.at[0, down_part(c), pl.ds(theirs, share)],
+            peer_down.at[down_part(c), :],
+        )
+    push("sn", slope_norm, peer_vec)
+    push("pn", param_norm, peer_gain)
+
+    sent = []
+
+    def share_norm(i):
+        for k in range(1, models):
+            copy = pltpu.make_async_remote_copy(
+                part.at[i],
+                got.at[i, k - 1],
+                norm_send.at[i, k - 1],
+                norm_recv.at[i, k - 1],
+                device_id={"model": lax.rem(spot + k, models)},
+                device_id_type=MESH,
+            )
+            copy.start()
+            sent.append((i, copy))
+
+    def whole_norm(i):
+        total = part[i]
+        for j, copy in sent:
+            if j == i:
+                copy.wait_recv()
+        for k in range(1, models):
+            total = total + got[i, k - 1]
+        return total
+
+    def row_squares(i, c, value):
+        @pl.loop(0, LANES // ROWS)
+        def _(r):
+            rows = pl.ds(c * LANES + r * ROWS, ROWS)
+            total = jnp.zeros((ROWS, LANES), f32)
+            for j in range(inner // LANES):
+                x = value(rows, pl.ds(j * LANES, LANES))
+                total = total + x * x
+            square[pl.ds(r * ROWS, ROWS), :] = total
+
+        part[i, :, c * LANES : (c + 1) * LANES] = jnp.sum(
+            square[...].T, axis=0, keepdims=True
+        )
+
+    def column_squares(c, value, totals):
+        def body(r, totals):
+            rows = pl.ds(c * down_rows + r * ROWS, ROWS)
+            out = []
+            for j, total in enumerate(totals):
+                x = value(rows, pl.ds(j * LANES, LANES))
+                x = x * x
+                for s in range(ROWS // 8):
+                    total = total + x[s * 8 : (s + 1) * 8]
+                out.append(total)
+            return tuple(out)
+
+        return lax.fori_loop(0, down_rows // ROWS, body, totals)
+
+    def zeros():
+        return tuple(jnp.zeros((8, LANES), f32) for _ in range(share // LANES))
+
+    def put_columns(i, totals):
+        for j, total in enumerate(totals):
+            part[i, :, j * LANES : (j + 1) * LANES] = jnp.sum(
+                total, axis=0, keepdims=True
+            )
+
+    def sum_up(rows, lanes):
+        return own_up[rows, lanes].astype(f32) + peer_up[rows, lanes].astype(f32)
+
+    def sum_down(rows, lanes):
+        return own_down[rows, lanes].astype(f32) + peer_down[rows, lanes].astype(f32)
+
+    loads["pu"].wait()
+    for c in range(up_chunks):
+        row_squares(0, c, lambda rows, lanes: next_up[rows, lanes])
+    share_norm(0)
+    loads["pd"].wait()
+    totals = zeros()
+    for c in range(down_chunks):
+        totals = column_squares(c, lambda rows, lanes: next_down[rows, lanes], totals)
+    put_columns(1, totals)
+    share_norm(1)
+
+    for c in range(up_chunks):
+        loads["up", c].wait()
+        pairs["up", c].wait_recv()
+        row_squares(2, c, lambda rows, lanes: sum_up(rows, lanes) * rate)
+    share_norm(2)
+
+    totals = zeros()
+    for c in range(down_chunks):
+        loads["down", c].wait()
+        pairs["down", c].wait_recv()
+        totals = column_squares(
+            c, lambda rows, lanes: sum_down(rows, lanes) * rate, totals
+        )
+    put_columns(3, totals)
+    share_norm(3)
+
+    loads["sn"].wait()
+    pairs["sn"].wait_recv()
+    pairs["pn"].wait_recv()
+    sum_vec[...] = (
+        (own_vec[...].astype(f32) + peer_vec[...].astype(f32)) * rate * learn_rate
+    )
+    new_gain = param_norm[...] - sum_vec[:, pl.ds(mine, share)]
+    next_norm[...] = new_gain
+    whole_vec[:, pl.ds(mine, share)] = new_gain
+    whole_vec[:, pl.ds(theirs, share)] = (
+        peer_gain[...] - sum_vec[:, pl.ds(theirs, share)]
+    )
+    half_norm[...] = whole_vec[...].astype(jnp.bfloat16)
+
+    ratio = jnp.sqrt(whole_norm(0)) * lax.rsqrt(whole_norm(2) + 1e-06)
+    ratio = ratio * (rate * learn_rate)
+    for c in range(up_chunks):
+        spread[...] = jnp.broadcast_to(
+            ratio[:, c * LANES : (c + 1) * LANES], (LANES, LANES)
+        ).T
+
+        @pl.loop(0, LANES // ROWS)
+        def _(r):
+            rows = pl.ds(c * LANES + r * ROWS, ROWS)
+            scale = spread[pl.ds(r * ROWS, ROWS), :]
+            for j in range(inner // LANES):
+                lanes = pl.ds(j * LANES, LANES)
+                new = next_up[rows, lanes] - sum_up(rows, lanes) * scale
+                next_up[rows, lanes] = new
+                half_up[pl.ds(mine + c * LANES + r * ROWS, ROWS), lanes] = new.astype(
+                    jnp.bfloat16
+                )
+
+        block = half_up.at[pl.ds(mine + c * LANES, LANES), :]
+        push(("half_up", c), block, block)
+
+    ratio = jnp.sqrt(whole_norm(1)) * lax.rsqrt(whole_norm(3) + 1e-06)
+    ratio = ratio * (rate * learn_rate)
+    scales = [
+        jnp.broadcast_to(ratio[:, j * LANES : (j + 1) * LANES], (ROWS, LANES))
+        for j in range(share // LANES)
+    ]
+    for c in range(down_chunks):
+
+        @pl.loop(0, down_rows // ROWS)
+        def _(r):
+            rows = pl.ds(c * down_rows + r * ROWS, ROWS)
+            for j, scale in enumerate(scales):
+                lanes = pl.ds(j * LANES, LANES)
+                new = next_down[rows, lanes] - sum_down(rows, lanes) * scale
+                next_down[rows, lanes] = new
+                half_down[rows, pl.ds(mine + j * LANES, LANES)] = new.astype(
+                    jnp.bfloat16
+                )
+
+        block = half_down.at[down_part(c), pl.ds(mine, share)]
+        push(("half_down", c), block, block)
+
+    for name, copy in pairs.items():
+        copy.wait_send()
+        if name[0] in ("half_up", "half_down"):
+            copy.wait_recv()
+    for _, copy in sent:
+        copy.wait_send()
+
+
+def fused(replicas, models, slope_up, slope_down, slope_norm, param_up, param_down, param_norm):
+    share, inner = param_up.shape
+    depth = param_down.shape[0]
+    width = slope_up.shape[1]
+    down_chunks = depth // (256 if depth % 256 == 0 else LANES)
+    up_chunks = share // LANES
+    moves = up_chunks + down_chunks + 2
+    bf16, f32 = jnp.bfloat16, jnp.float32
+    hbm = pl.BlockSpec(memory_space=pltpu.HBM)
+    vmem = pl.BlockSpec(memory_space=pltpu.VMEM)
+    outs = pl.pallas_call(
+        functools.partial(update_kernel, replicas, models),
+        out_shape=(
+            OUT((width, inner), bf16),
+            OUT((depth, width), bf16),
+            OUT((1, width), bf16),
+            OUT((share, inner), f32),
+            OUT((depth, share), f32),
+            OUT((1, share), f32),
+        ),
+        in_specs=[hbm] * 5 + [vmem],
+        out_specs=(vmem,) * 6,
+        scratch_shapes=[
+            pltpu.VMEM((share, inner), bf16),
+            pltpu.VMEM((share, inner), bf16),
+            pltpu.VMEM((depth, share), bf16),
+            pltpu.VMEM((depth, share), bf16),
+            pltpu.VMEM((1, width), bf16),
+            pltpu.VMEM((1, width), bf16),
+            pltpu.VMEM((1, share), f32),
+            pltpu.VMEM((1, width), f32),
+            pltpu.VMEM((1, width), f32),
+            pltpu.VMEM((4, 1, share), f32),
+            pltpu.VMEM((4, models - 1, 1, share), f32),
+            pltpu.VMEM((LANES, LANES), f32),
+            pltpu.VMEM((LANES, LANES), f32),
+            pltpu.SemaphoreType.DMA((moves + 1,)),
+            pltpu.SemaphoreType.DMA((2 * moves,)),
+            pltpu.SemaphoreType.DMA((2 * moves,)),
+            pltpu.SemaphoreType.DMA((4, models - 1)),
+            pltpu.SemaphoreType.DMA((4, models - 1)),
+        ],
+        compiler_params=pltpu.CompilerParams(
+            collective_id=0, has_side_effects=True, vmem_limit_bytes=24 * 2**20
+        ),
+    )(
+        *(
+            pltpu.with_memory_space_constraint(x, pltpu.HBM)
+            for x in (slope_up, slope_down, slope_norm, param_up, param_down)
+        ),
+        param_norm[None],
+    )
+    half_up, half_down, half_norm, next_up, next_down, next_norm = outs
+    return half_up, half_down, half_norm[0], next_up, next_down, next_norm[0]
+
+
+def suits(mesh, *arrays):
+    slope_up, param_up, param_down = arrays
+    return (
+        mesh.shape["replica"] == 2
+        and mesh.shape["model"] > 1
+        and param_up.shape[0] % LANES == 0
+        and param_up.shape[1] % LANES == 0
+        and param_down.shape[0] % LANES == 0
+    )
+
+
+def step(mesh, slope_up, slope_down, slope_norm, param_up, param_down, param_norm):
+    args = (slope_up, slope_down, slope_norm, param_up, param_down, param_norm)
+    if suits(mesh, slope_up, param_up, param_down):
+        return fused(mesh.shape["replica"], mesh.shape["model"], *args)
+    return shards(*args)
+
+
+OUT = pltpu.VMEM
+
+
 def solution(mesh):
     return jax.shard_map(
-        shards,
+        functools.partial(step, mesh),
         mesh=mesh,
         in_specs=(
             P(("copy", "replica"), None, "model"),

time: 105 us -> 26.4 us (0.25)
  waiting for transfers between devices: 39.4 us -> 0 us
  blocking collectives: 20.6 us -> 0 us
  Pallas kernels: 0 us -> 16.8 us
  other arithmetic: 15.5 us -> 1.22 us
  between operations: 13.9 us -> 0.64 us
  local copies, waits for them, and re-layouts: 14.9 us -> 7.52 us
    psum x2 -> x0, blocking collectives: 18.8 us -> none  [the longest x1 16.3 us: shards(): lax.psum((jnp.sum(param_up * param_up, axis=1, keepdims=True), jnp.sum(pa...]
    pallas_call x0 -> x1, Pallas kernels: none -> 16.8 us  [fused(): pl.pallas_call(functools.partial(update_kernel, replicas, models), out_sh...]
    all_gather x2 -> x0, waiting for transfers between devices: 16.5 us -> none  [the longest x1 15.5 us: shards(): lax.all_gather(next_up.astype(jnp.bfloat16), 'replica', axis=0, tiled=True)]
    reduce_scatter x1 -> x0, waiting for transfers between devices: 11.6 us -> none  [shards(): lax.psum_scatter(slope_up[0].astype(jnp.float32).astype(jnp.bfloat16), 'r...]
    unnamed x5 -> x0, waiting for transfers between devices: 11.4 us -> none
    convert_element_type x4 -> x0, other arithmetic: 10.2 us -> none  [the longest x1 4.78 us: shards(): next_down.astype(jnp.bfloat16)]
    unnamed x16 -> x4, local copies, waits for them, and re-layouts: 14.8 us -> 6.83 us
    reduce_sum x4 -> x0, other arithmetic: 5.18 us -> none  [the longest x1 2.45 us: shards(): jnp.sum(param_up * param_up, axis=1, keepdims=True)]
  transfers between devices with their start and end apart: 4 -> 0, of which waited for: 4 -> 0; matrix products, arithmetic and copies ran while one was open for 12% -> 0% of each run, Pallas kernels for 0% -> 0%
where the time goes in v1:
time: 26.4 us; the launch traced here: 26.2 us
  Pallas kernels  16.8 us (64%)
  local copies, waits for them, and re-layouts  7.52 us (28%)
  other arithmetic  1.22 us (5%)
  between operations  0.64 us (2%)
    pallas_call x1, Pallas kernels, fused(): pl.pallas_call(functools.partial(update_kernel, replicas, models), out_sh...  16.8 us
    unnamed x4, local copies, waits for them, and re-layouts  6.83 us
    pallas_call x2, other arithmetic, fused(): pl.pallas_call(functools.partial(update_kernel, replicas, models), out_sh...  1.22 us
    broadcast_in_dim x1, local copies, waits for them, and re-layouts, fused(): param_norm[None]  0.69 us

profile of v1, /device:TPU:0, one launch (start us, length us, event | category | flops | bytes accessed | tf_op | source)
XLA Modules:
  0.0 26.2 jit_solution(13092933361460897445)
XLA Ops:
  0.6 0.7 %broadcast_in_dim.3.param_norm = f32[1,640]{1,0:T(1,128)S(1)} reshape(f32[640]{0:T(1024)} %param.11) | data formatting | bytes 5120 | tf_op jit(solution)/shard_map/broadcast_in_dim | solution.py:392
  1.3 16.8 %shard_map.109 = (bf16[1280,1280]{1,0:T(8,128)(2,1)S(1)}, bf16[1280,1280]{1,0:T(8,128)(2,1)S(1)}, bf16[1,1280]{1,0:T(2,128)(2,1)S(1)}, f32[640,1280]{1,0:T(8,128...) custom-call(bf16[1,1280,1280]{2,1,0:T(8,128)(2,1)} %slope_up.1, bf16[1,1280,1280]{2,1,0:T(8,128)(2,1)} %slope_down.1, ...), custom_call_target="tpu_custom_call" | custom-call | tf_op jit(solution)/shard_map/pallas_call | solution.py:352
  18.1 1.7 %copy.16 = bf16[1280,1280]{1,0:T(8,128)(2,1)} copy(bf16[1280,1280]{1,0:T(8,128)(2,1)S(1)} %get-tuple-element.18) | data formatting | bytes 6553600
  19.8 1.7 %copy.17 = bf16[1280,1280]{1,0:T(8,128)(2,1)} copy(bf16[1280,1280]{1,0:T(8,128)(2,1)S(1)} %get-tuple-element.19) | data formatting | bytes 6553600
  21.5 1.7 %copy.18 = f32[640,1280]{1,0:T(8,128)} copy(f32[640,1280]{1,0:T(8,128)S(1)} %get-tuple-element.21) | data formatting | bytes 6553600
  23.2 1.7 %copy.19 = f32[1280,640]{1,0:T(8,128)} copy(f32[1280,640]{1,0:T(8,128)S(1)} %get-tuple-element.22) | data formatting | bytes 6553600
  24.9 0.6 %reduce = bf16[1280]{0:T(1024)(128)(2,1)} reduce(bf16[1,1280]{1,0:T(2,128)(2,1)S(1)} %get-tuple-element.14, bf16[]{:T(256)} %constant.3), dimensions={0}, to_apply=%get-tuple-element.14.reduce_sub_computation | reduce | bytes 5122 | tf_op jit(solution)/shard_map/pallas_call | solution.py:352
  25.6 0.6 %reduce.1 = f32[640]{0:T(1024)} reduce(f32[1,640]{1,0:T(1,128)S(1)} %get-tuple-element.17, f32[]{:T(128)} %constant.4), dimensions={0}, to_apply=%get-tuple-element.17.reduce_sub_computation | reduce | bytes 5124 | tf_op jit(solution)/shard_map/pallas_call | solution.py:352

commit v2 on v1

--- a/solution.py
+++ b/solution.py
@@ -82,9 +82,9 @@
     peer_down,
     own_vec,
     peer_vec,
+    own_gain,
     peer_gain,
     sum_vec,
-    whole_vec,
     part,
     got,
     square,
@@ -150,6 +150,7 @@
             own_down.at[down_part(c), :],
         )
     load("sn", slope_norm, own_vec)
+    load("pn", param_norm, own_gain)
 
     barrier = pltpu.get_barrier_semaphore()
     pl.semaphore_signal(
@@ -274,18 +275,18 @@
     share_norm(3)
 
     loads["sn"].wait()
+    loads["pn"].wait()
     pairs["sn"].wait_recv()
     pairs["pn"].wait_recv()
     sum_vec[...] = (
         (own_vec[...].astype(f32) + peer_vec[...].astype(f32)) * rate * learn_rate
     )
-    new_gain = param_norm[...] - sum_vec[:, pl.ds(mine, share)]
+    new_gain = own_gain[...].reshape(1, share) - sum_vec[:, pl.ds(mine, share)]
     next_norm[...] = new_gain
-    whole_vec[:, pl.ds(mine, share)] = new_gain
-    whole_vec[:, pl.ds(theirs, share)] = (
-        peer_gain[...] - sum_vec[:, pl.ds(theirs, share)]
-    )
-    half_norm[...] = whole_vec[...].astype(jnp.bfloat16)
+    half_norm[:, pl.ds(mine, share)] = new_gain
+    half_norm[:, pl.ds(theirs, share)] = (
+        peer_gain[...].reshape(1, share) - sum_vec[:, pl.ds(theirs, share)]
+    )
 
     ratio = jnp.sqrt(whole_norm(0)) * lax.rsqrt(whole_norm(2) + 1e-06)
     ratio = ratio * (rate * learn_rate)
@@ -337,6 +338,41 @@
             copy.wait_recv()
     for _, copy in sent:
         copy.wait_send()
+
+
+def write_kernel(
+    half_up,
+    half_down,
+    half_norm,
+    next_up,
+    next_down,
+    next_norm,
+    half_up_out,
+    half_down_out,
+    half_norm_out,
+    next_up_out,
+    next_down_out,
+    next_norm_out,
+    sem,
+):
+    moves = (
+        (half_up, half_up_out),
+        (half_down, half_down_out),
+        (next_up, next_up_out),
+        (next_down, next_down_out),
+    )
+    copies = [
+        pltpu.make_async_copy(source, target, sem.at[i])
+        for i, (source, target) in enumerate(moves)
+    ]
+    for copy in copies:
+        copy.start()
+    half_norm_out[...] = half_norm[...].reshape(half_norm_out.shape).astype(
+        jnp.bfloat16
+    )
+    next_norm_out[...] = next_norm[...].reshape(next_norm_out.shape)
+    for copy in copies:
+        copy.wait()
 
 
 def fused(replicas, models, slope_up, slope_down, slope_norm, param_up, param_down, param_norm):
@@ -354,12 +390,12 @@
         out_shape=(
             OUT((width, inner), bf16),
             OUT((depth, width), bf16),
-            OUT((1, width), bf16),
+            OUT((1, width), f32),
             OUT((share, inner), f32),
             OUT((depth, share), f32),
             OUT((1, share), f32),
         ),
-        in_specs=[hbm] * 5 + [vmem],
+        in_specs=[hbm] * 6,
         out_specs=(vmem,) * 6,
         scratch_shapes=[
             pltpu.VMEM((share, inner), bf16),
@@ -368,14 +404,14 @@
             pltpu.VMEM((depth, share), bf16),
             pltpu.VMEM((1, width), bf16),
             pltpu.VMEM((1, width), bf16),
-            pltpu.VMEM((1, share), f32),
-            pltpu.VMEM((1, width), f32),
+            pltpu.VMEM((share,), f32),
+            pltpu.VMEM((share,), f32),
             pltpu.VMEM((1, width), f32),
             pltpu.VMEM((4, 1, share), f32),
             pltpu.VMEM((4, models - 1, 1, share), f32),
             pltpu.VMEM((LANES, LANES), f32),
             pltpu.VMEM((LANES, LANES), f32),
-            pltpu.SemaphoreType.DMA((moves + 1,)),
+            pltpu.SemaphoreType.DMA((moves + 2,)),
             pltpu.SemaphoreType.DMA((2 * moves,)),
             pltpu.SemaphoreType.DMA((2 * moves,)),
             pltpu.SemaphoreType.DMA((4, models - 1)),
@@ -387,12 +423,26 @@
     )(
         *(
             pltpu.with_memory_space_constraint(x, pltpu.HBM)
-            for x in (slope_up, slope_down, slope_norm, param_up, param_down)
-        ),
-        param_norm[None],
-    )
-    half_up, half_down, half_norm, next_up, next_down, next_norm = outs
-    return half_up, half_down, half_norm[0], next_up, next_down, next_norm[0]
+            for x in (
+                slope_up, slope_down, slope_norm, param_up, param_down, param_norm
+            )
+        )
+    )
+    return pl.pallas_call(
+        write_kernel,
+        out_shape=(
+            jax.ShapeDtypeStruct((width, inner), bf16),
+            jax.ShapeDtypeStruct((depth, width), bf16),
+            jax.ShapeDtypeStruct((width,), bf16),
+            jax.ShapeDtypeStruct((share, inner), f32),
+            jax.ShapeDtypeStruct((depth, share), f32),
+            jax.ShapeDtypeStruct((share,), f32),
+        ),
+        in_specs=[vmem] * 6,
+        out_specs=(hbm, hbm, vmem, hbm, hbm, vmem),
+        scratch_shapes=[pltpu.SemaphoreType.DMA((4,))],
+        compiler_params=pltpu.CompilerParams(vmem_limit_bytes=24 * 2**20),
+    )(*(pltpu.with_memory_space_constraint(x, pltpu.VMEM) for x in outs))
 
 
 def suits(mesh, *arrays):

time: 26.4 us -> 23.1 us (0.88)
  local copies, waits for them, and re-layouts: 7.52 us -> 0 us
  Pallas kernels: 16.8 us -> 22.3 us
  other arithmetic: 1.22 us -> 0 us
    unnamed x4 -> x0, local copies, waits for them, and re-layouts: 6.83 us -> none
    pallas_call x0 -> x1, Pallas kernels: none -> 5.47 us  [fused(): pl.pallas_call(write_kernel, out_shape=(jax.ShapeDtypeStruct((width, inne...]
    pallas_call x2 -> x0, other arithmetic: 1.22 us -> none  [fused(): pl.pallas_call(functools.partial(update_kernel, replicas, models), out_sh...]
    broadcast_in_dim x1 -> x0, local copies, waits for them, and re-layouts: 0.69 us -> none  [fused(): param_norm[None]]
where the time goes in v2:
time: 23.1 us; the launch traced here: 22.9 us
  Pallas kernels  22.3 us (97%)
  between operations  0.64 us (3%)
    pallas_call x1, Pallas kernels, fused(): pl.pallas_call(functools.partial(update_kernel, replicas, models), out_sh...  16.8 us
    pallas_call x1, Pallas kernels, fused(): pl.pallas_call(write_kernel, out_shape=(jax.ShapeDtypeStruct((width, inne...  5.47 us

profile of v2, /device:TPU:0, one launch (start us, length us, event | category | flops | bytes accessed | tf_op | source)
XLA Modules:
  0.0 22.9 jit_solution(8193581906202682639)
XLA Ops:
  0.6 16.8 %shard_map.109 = (bf16[1280,1280]{1,0:T(8,128)(2,1)S(1)}, bf16[1280,1280]{1,0:T(8,128)(2,1)S(1)}, f32[1,1280]{1,0:T(1,128)S(1)}, f32[640,1280]{1,0:T(8,128)S(1)}...) custom-call(bf16[1,1280,1280]{2,1,0:T(8,128)(2,1)} %slope_up.1, bf16[1,1280,1280]{2,1,0:T(8,128)(2,1)} %slope_down.1, ...), custom_call_target="tpu_custom_call" | custom-call | tf_op jit(solution)/shard_map/pallas_call | solution.py:388
  17.5 5.5 %shard_map.110 = (bf16[1280,1280]{1,0:T(8,128)(2,1)}, bf16[1280,1280]{1,0:T(8,128)(2,1)}, bf16[1280]{0:T(1024)(128)(2,1)}, f32[640,1280]{1,0:T(8,128)}, f32[1280,640]{1,0:T(8,128)}, /*index=5*/f32[640]{0:T(1024)}) custom-call(bf16[1280,1280]{1,0:T(8,128)(2,1)S(1)} %get-tuple-element.12.half_up, bf16[1280,1280]{1,0:T(8,128)(2,1)S(1)} %get-tuple-element.13.half_down, ...), custom_call_target="tpu_custom_call" | custom-call | tf_op jit(solution)/shard_map/pallas_call | solution.py:431

commit v3 on v2

--- a/solution.py
+++ b/solution.py
@@ -59,6 +59,7 @@
 MESH = pl.DeviceIdType.MESH
 LANES = 128
 ROWS = 32
+AHEAD = 6
 
 
 def update_kernel(
@@ -87,6 +88,8 @@
     sum_vec,
     part,
     got,
+    piece,
+    got_piece,
     square,
     spread,
     load_sem,
@@ -94,6 +97,8 @@
     pair_recv,
     norm_send,
     norm_recv,
+    piece_send,
+    piece_recv,
 ):
     me = lax.axis_index("replica")
     other = 1 - me
@@ -101,8 +106,8 @@
     share, inner = param_up.shape
     depth = param_down.shape[0]
     up_chunks = share // LANES
-    down_rows = 256 if depth % 256 == 0 else LANES
-    down_chunks = depth // down_rows
+    down_chunks = share // LANES
+    down_rows = 4 * ROWS
     mine = pl.multiple_of(me * share, LANES)
     theirs = pl.multiple_of(other * share, LANES)
     rate = replicas ** (-0.5)
@@ -133,7 +138,7 @@
         return pl.ds(c * LANES, LANES)
 
     def down_part(c):
-        return pl.ds(c * down_rows, down_rows)
+        return pl.ds(c * LANES, LANES)
 
     load("pu", param_up, next_up)
     load("pd", param_down, next_down)
@@ -146,8 +151,8 @@
     for c in range(down_chunks):
         load(
             ("down", c),
-            slope_down.at[0, down_part(c), pl.ds(mine, share)],
-            own_down.at[down_part(c), :],
+            slope_down.at[0, :, pl.ds(mine + c * LANES, LANES)],
+            own_down.at[:, down_part(c)],
         )
     load("sn", slope_norm, own_vec)
     load("pn", param_norm, own_gain)
@@ -174,37 +179,46 @@
     for c in range(down_chunks):
         push(
             ("down", c),
-            slope_down.at[0, down_part(c), pl.ds(theirs, share)],
-            peer_down.at[down_part(c), :],
+            slope_down.at[0, :, pl.ds(theirs + c * LANES, LANES)],
+            peer_down.at[:, down_part(c)],
         )
     push("sn", slope_norm, peer_vec)
     push("pn", param_norm, peer_gain)
 
     sent = []
 
-    def share_norm(i):
+    def share_norm(source, target, sems, i):
+        copies = []
         for k in range(1, models):
             copy = pltpu.make_async_remote_copy(
-                part.at[i],
-                got.at[i, k - 1],
-                norm_send.at[i, k - 1],
-                norm_recv.at[i, k - 1],
+                source.at[i],
+                target.at[i, k - 1],
+                sems[0].at[i, k - 1],
+                sems[1].at[i, k - 1],
                 device_id={"model": lax.rem(spot + k, models)},
                 device_id_type=MESH,
             )
             copy.start()
-            sent.append((i, copy))
-
-    def whole_norm(i):
-        total = part[i]
-        for j, copy in sent:
-            if j == i:
+            copies.append(copy)
+        sent.extend(copies)
+
+        def whole():
+            for copy in copies:
                 copy.wait_recv()
-        for k in range(1, models):
-            total = total + got[i, k - 1]
-        return total
-
-    def row_squares(i, c, value):
+            total = source[i]
+            for k in range(1, models):
+                total = total + target[i, k - 1]
+            return total
+
+        return whole
+
+    def share_param(i):
+        return share_norm(part, got, (norm_send, norm_recv), i)
+
+    def share_slope(i):
+        return share_norm(piece, got_piece, (piece_send, piece_recv), i)
+
+    def row_squares(c, value):
         @pl.loop(0, LANES // ROWS)
         def _(r):
             rows = pl.ds(c * LANES + r * ROWS, ROWS)
@@ -214,32 +228,19 @@
                 total = total + x * x
             square[pl.ds(r * ROWS, ROWS), :] = total
 
-        part[i, :, c * LANES : (c + 1) * LANES] = jnp.sum(
-            square[...].T, axis=0, keepdims=True
-        )
-
-    def column_squares(c, value, totals):
-        def body(r, totals):
-            rows = pl.ds(c * down_rows + r * ROWS, ROWS)
-            out = []
-            for j, total in enumerate(totals):
-                x = value(rows, pl.ds(j * LANES, LANES))
-                x = x * x
-                for s in range(ROWS // 8):
-                    total = total + x[s * 8 : (s + 1) * 8]
-                out.append(total)
-            return tuple(out)
-
-        return lax.fori_loop(0, down_rows // ROWS, body, totals)
-
-    def zeros():
-        return tuple(jnp.zeros((8, LANES), f32) for _ in range(share // LANES))
-
-    def put_columns(i, totals):
-        for j, total in enumerate(totals):
-            part[i, :, j * LANES : (j + 1) * LANES] = jnp.sum(
-                total, axis=0, keepdims=True
-            )
+        return jnp.sum(square[...].T, axis=0, keepdims=True)
+
+    def column_squares(c, value):
+        def body(r, total):
+            for q in range(down_rows // ROWS):
+                x = value(pl.ds(r * down_rows + q * ROWS, ROWS), down_part(c))
+                total = total + x * x
+            return total
+
+        total = lax.fori_loop(
+            0, depth // down_rows, body, jnp.zeros((ROWS, LANES), f32)
+        )
+        return jnp.sum(total, axis=0, keepdims=True)
 
     def sum_up(rows, lanes):
         return own_up[rows, lanes].astype(f32) + peer_up[rows, lanes].astype(f32)
@@ -249,51 +250,49 @@
 
     loads["pu"].wait()
     for c in range(up_chunks):
-        row_squares(0, c, lambda rows, lanes: next_up[rows, lanes])
-    share_norm(0)
+        part[0, :, c * LANES : (c + 1) * LANES] = row_squares(
+            c, lambda rows, lanes: next_up[rows, lanes]
+        )
+    whole_up = share_param(0)
     loads["pd"].wait()
-    totals = zeros()
     for c in range(down_chunks):
-        totals = column_squares(c, lambda rows, lanes: next_down[rows, lanes], totals)
-    put_columns(1, totals)
-    share_norm(1)
-
-    for c in range(up_chunks):
-        loads["up", c].wait()
-        pairs["up", c].wait_recv()
-        row_squares(2, c, lambda rows, lanes: sum_up(rows, lanes) * rate)
-    share_norm(2)
-
-    totals = zeros()
-    for c in range(down_chunks):
-        loads["down", c].wait()
-        pairs["down", c].wait_recv()
-        totals = column_squares(
-            c, lambda rows, lanes: sum_down(rows, lanes) * rate, totals
-        )
-    put_columns(3, totals)
-    share_norm(3)
-
-    loads["sn"].wait()
-    loads["pn"].wait()
-    pairs["sn"].wait_recv()
-    pairs["pn"].wait_recv()
-    sum_vec[...] = (
-        (own_vec[...].astype(f32) + peer_vec[...].astype(f32)) * rate * learn_rate
-    )
-    new_gain = own_gain[...].reshape(1, share) - sum_vec[:, pl.ds(mine, share)]
-    next_norm[...] = new_gain
-    half_norm[:, pl.ds(mine, share)] = new_gain
-    half_norm[:, pl.ds(theirs, share)] = (
-        peer_gain[...].reshape(1, share) - sum_vec[:, pl.ds(theirs, share)]
-    )
-
-    ratio = jnp.sqrt(whole_norm(0)) * lax.rsqrt(whole_norm(2) + 1e-06)
-    ratio = ratio * (rate * learn_rate)
-    for c in range(up_chunks):
-        spread[...] = jnp.broadcast_to(
-            ratio[:, c * LANES : (c + 1) * LANES], (LANES, LANES)
-        ).T
+        part[1, :, c * LANES : (c + 1) * LANES] = column_squares(
+            c, lambda rows, lanes: next_down[rows, lanes]
+        )
+    whole_down = share_param(1)
+
+    pieces = [("up", c) for c in range(up_chunks)]
+    pieces += [("down", c) for c in range(down_chunks)]
+    slope_wholes = {}
+    param_wholes = {}
+
+    def measure_piece(n):
+        kind, c = pieces[n]
+        loads[pieces[n]].wait()
+        pairs[pieces[n]].wait_recv()
+        if kind == "up":
+            piece[n] = row_squares(c, lambda rows, lanes: sum_up(rows, lanes) * rate)
+        else:
+            piece[n] = column_squares(
+                c, lambda rows, lanes: sum_down(rows, lanes) * rate
+            )
+        slope_wholes[n] = share_slope(n)
+
+    def update_piece(n):
+        kind, c = pieces[n]
+        if kind not in param_wholes:
+            total = (whole_up if kind == "up" else whole_down)()
+            param_wholes[kind] = jnp.sqrt(total) * (rate * learn_rate)
+        ratio = param_wholes[kind][:, c * LANES : (c + 1) * LANES] * lax.rsqrt(
+            slope_wholes[n]() + 1e-06
+        )
+        if kind == "up":
+            update_up(c, ratio)
+        else:
+            update_down(c, ratio)
+
+    def update_up(c, ratio):
+        spread[...] = jnp.broadcast_to(ratio, (LANES, LANES)).T
 
         @pl.loop(0, LANES // ROWS)
         def _(r):
@@ -310,33 +309,48 @@
         block = half_up.at[pl.ds(mine + c * LANES, LANES), :]
         push(("half_up", c), block, block)
 
-    ratio = jnp.sqrt(whole_norm(1)) * lax.rsqrt(whole_norm(3) + 1e-06)
-    ratio = ratio * (rate * learn_rate)
-    scales = [
-        jnp.broadcast_to(ratio[:, j * LANES : (j + 1) * LANES], (ROWS, LANES))
-        for j in range(share // LANES)
-    ]
-    for c in range(down_chunks):
-
-        @pl.loop(0, down_rows // ROWS)
+    def update_down(c, ratio):
+        scale = jnp.broadcast_to(ratio, (ROWS, LANES))
+        lanes = down_part(c)
+        place = pl.ds(mine + c * LANES, LANES)
+
+        @pl.loop(0, depth // down_rows)
         def _(r):
-            rows = pl.ds(c * down_rows + r * ROWS, ROWS)
-            for j, scale in enumerate(scales):
-                lanes = pl.ds(j * LANES, LANES)
+            for q in range(down_rows // ROWS):
+                rows = pl.ds(r * down_rows + q * ROWS, ROWS)
                 new = next_down[rows, lanes] - sum_down(rows, lanes) * scale
                 next_down[rows, lanes] = new
-                half_down[rows, pl.ds(mine + j * LANES, LANES)] = new.astype(
-                    jnp.bfloat16
-                )
-
-        block = half_down.at[down_part(c), pl.ds(mine, share)]
+                half_down[rows, place] = new.astype(jnp.bfloat16)
+
+        block = half_down.at[:, place]
         push(("half_down", c), block, block)
+
+    ahead = min(AHEAD, len(pieces))
+    for n in range(len(pieces) + ahead):
+        if n < len(pieces):
+            measure_piece(n)
+        if n >= ahead:
+            update_piece(n - ahead)
+
+    loads["sn"].wait()
+    loads["pn"].wait()
+    pairs["sn"].wait_recv()
+    pairs["pn"].wait_recv()
+    sum_vec[...] = (
+        (own_vec[...].astype(f32) + peer_vec[...].astype(f32)) * rate * learn_rate
+    )
+    new_gain = own_gain[...].reshape(1, share) - sum_vec[:, pl.ds(mine, share)]
+    next_norm[...] = new_gain
+    half_norm[:, pl.ds(mine, share)] = new_gain
+    half_norm[:, pl.ds(theirs, share)] = (
+        peer_gain[...].reshape(1, share) - sum_vec[:, pl.ds(theirs, share)]
+    )
 
     for name, copy in pairs.items():
         copy.wait_send()
         if name[0] in ("half_up", "half_down"):
             copy.wait_recv()
-    for _, copy in sent:
+    for copy in sent:
         copy.wait_send()
 
 
@@ -379,7 +393,7 @@
     share, inner = param_up.shape
     depth = param_down.shape[0]
     width = slope_up.shape[1]
-    down_chunks = depth // (256 if depth % 256 == 0 else LANES)
+    down_chunks = share // LANES
     up_chunks = share // LANES
     moves = up_chunks + down_chunks + 2
     bf16, f32 = jnp.bfloat16, jnp.float32
@@ -407,15 +421,19 @@
             pltpu.VMEM((share,), f32),
             pltpu.VMEM((share,), f32),
             pltpu.VMEM((1, width), f32),
-            pltpu.VMEM((4, 1, share), f32),
-            pltpu.VMEM((4, models - 1, 1, share), f32),
+            pltpu.VMEM((2, 1, share), f32),
+            pltpu.VMEM((2, models - 1, 1, share), f32),
+            pltpu.VMEM((moves - 2, 1, LANES), f32),
+            pltpu.VMEM((moves - 2, models - 1, 1, LANES), f32),
             pltpu.VMEM((LANES, LANES), f32),
             pltpu.VMEM((LANES, LANES), f32),
             pltpu.SemaphoreType.DMA((moves + 2,)),
             pltpu.SemaphoreType.DMA((2 * moves,)),
             pltpu.SemaphoreType.DMA((2 * moves,)),
-            pltpu.SemaphoreType.DMA((4, models - 1)),
-            pltpu.SemaphoreType.DMA((4, models - 1)),
+            pltpu.SemaphoreType.DMA((2, models - 1)),
+            pltpu.SemaphoreType.DMA((2, models - 1)),
+            pltpu.SemaphoreType.DMA((moves - 2, models - 1)),
+            pltpu.SemaphoreType.DMA((moves - 2, models - 1)),
         ],
         compiler_params=pltpu.CompilerParams(
             collective_id=0, has_side_effects=True, vmem_limit_bytes=24 * 2**20

time: 23.1 us -> 22.5 us (0.974)
  Pallas kernels: 22.3 us -> 21.7 us
    pallas_call x1, Pallas kernels: 16.8 us -> 16.3 us  [fused(): pl.pallas_call(functools.partial(update_kernel, replicas, models), out_sh...]
where the time goes in v3:
time: 22.5 us; the launch traced here: 22.4 us
  Pallas kernels  21.7 us (96%)
  between operations  0.64 us (3%)
    pallas_call x1, Pallas kernels, fused(): pl.pallas_call(functools.partial(update_kernel, replicas, models), out_sh...  16.3 us
    pallas_call x1, Pallas kernels, fused(): pl.pallas_call(write_kernel, out_shape=(jax.ShapeDtypeStruct((width, inne...  5.47 us

profile of v3, /device:TPU:0, one launch (start us, length us, event | category | flops | bytes accessed | tf_op | source)
XLA Modules:
  0.0 22.4 jit_solution(3603717460998926779)
XLA Ops:
  0.6 16.3 %shard_map.109 = (bf16[1280,1280]{1,0:T(8,128)(2,1)S(1)}, bf16[1280,1280]{1,0:T(8,128)(2,1)S(1)}, f32[1,1280]{1,0:T(1,128)S(1)}, f32[640,1280]{1,0:T(8,128)S(1)}...) custom-call(bf16[1,1280,1280]{2,1,0:T(8,128)(2,1)} %slope_up.1, bf16[1,1280,1280]{2,1,0:T(8,128)(2,1)} %slope_down.1, ...), custom_call_target="tpu_custom_call" | custom-call | tf_op jit(solution)/shard_map/pallas_call | solution.py:402
  16.9 5.5 %shard_map.110 = (bf16[1280,1280]{1,0:T(8,128)(2,1)}, bf16[1280,1280]{1,0:T(8,128)(2,1)}, bf16[1280]{0:T(1024)(128)(2,1)}, f32[640,1280]{1,0:T(8,128)}, f32[1280,640]{1,0:T(8,128)}, /*index=5*/f32[640]{0:T(1024)}) custom-call(bf16[1280,1280]{1,0:T(8,128)(2,1)S(1)} %get-tuple-element.12.half_up, bf16[1280,1280]{1,0:T(8,128)(2,1)S(1)} %get-tuple-element.13.half_down, ...), custom_call_target="tpu_custom_call" | custom-call | tf_op jit(solution)/shard_map/pallas_call | solution.py:449

commit v4 on v3

--- a/solution.py
+++ b/solution.py
@@ -254,12 +254,14 @@
             c, lambda rows, lanes: next_up[rows, lanes]
         )
     whole_up = share_param(0)
-    loads["pd"].wait()
-    for c in range(down_chunks):
-        part[1, :, c * LANES : (c + 1) * LANES] = column_squares(
-            c, lambda rows, lanes: next_down[rows, lanes]
-        )
-    whole_down = share_param(1)
+
+    def measure_down():
+        loads["pd"].wait()
+        for c in range(down_chunks):
+            part[1, :, c * LANES : (c + 1) * LANES] = column_squares(
+                c, lambda rows, lanes: next_down[rows, lanes]
+            )
+        return share_param(1)
 
     pieces = [("up", c) for c in range(up_chunks)]
     pieces += [("down", c) for c in range(down_chunks)]
@@ -327,6 +329,8 @@
 
     ahead = min(AHEAD, len(pieces))
     for n in range(len(pieces) + ahead):
+        if n == 2:
+            whole_down = measure_down()
         if n < len(pieces):
             measure_piece(n)
         if n >= ahead:

time: 22.5 us -> 22.1 us (0.982)
  Pallas kernels: 21.7 us -> 21.3 us
    pallas_call x1, Pallas kernels: 16.3 us -> 15.9 us  [fused(): pl.pallas_call(functools.partial(update_kernel, replicas, models), out_sh...]
where the time goes in v4:
time: 22.1 us; the launch traced here: 22 us
  Pallas kernels  21.3 us (96%)
  between operations  0.64 us (3%)
    pallas_call x1, Pallas kernels, fused(): pl.pallas_call(functools.partial(update_kernel, replicas, models), out_sh...  15.9 us
    pallas_call x1, Pallas kernels, fused(): pl.pallas_call(write_kernel, out_shape=(jax.ShapeDtypeStruct((width, inne...  5.47 us

profile of v4, /device:TPU:0, one launch (start us, length us, event | category | flops | bytes accessed | tf_op | source)
XLA Modules:
  0.0 22.0 jit_solution(14531814747231090303)
XLA Ops:
  0.6 15.9 %shard_map.109 = (bf16[1280,1280]{1,0:T(8,128)(2,1)S(1)}, bf16[1280,1280]{1,0:T(8,128)(2,1)S(1)}, f32[1,1280]{1,0:T(1,128)S(1)}, f32[640,1280]{1,0:T(8,128)S(1)}...) custom-call(bf16[1,1280,1280]{2,1,0:T(8,128)(2,1)} %slope_up.1, bf16[1,1280,1280]{2,1,0:T(8,128)(2,1)} %slope_down.1, ...), custom_call_target="tpu_custom_call" | custom-call | tf_op jit(solution)/shard_map/pallas_call | solution.py:406
  16.5 5.5 %shard_map.110 = (bf16[1280,1280]{1,0:T(8,128)(2,1)}, bf16[1280,1280]{1,0:T(8,128)(2,1)}, bf16[1280]{0:T(1024)(128)(2,1)}, f32[640,1280]{1,0:T(8,128)}, f32[1280,640]{1,0:T(8,128)}, /*index=5*/f32[640]{0:T(1024)}) custom-call(bf16[1280,1280]{1,0:T(8,128)(2,1)S(1)} %get-tuple-element.12.half_up, bf16[1280,1280]{1,0:T(8,128)(2,1)S(1)} %get-tuple-element.13.half_down, ...), custom_call_target="tpu_custom_call" | custom-call | tf_op jit(solution)/shard_map/pallas_call | solution.py:453
